TPU v7x, 32 devices: a whole 2x2x4 slice. The times are simulated.
32 devices in a mesh: samp: 8 (over z, x), feat: 4 (over y, core).
Axes of the slice: x: 2, y: 2, z: 4, core: 2. Of those that a mesh axis runs over, the one named last changes fastest.
Arguments:
- features: bfloat16 [131072, 2048], P('samp', 'feat'), may hold values from -40 to 40
- labels: int32 [131072], P('samp'), may hold values from 0 to 9
- weights: float32 [10, 2048], P(None, 'feat'), may hold values from -6 to 6
- sketch_basis: float32 [10, 2048, 512], P(None, 'feat'), may hold values from -0.0390625 to 0.0390625
- sketch_values: float32 [512], replicated, may hold values from 0.05 to 2
Outputs:
- newton_step: float32 [10, 2048], P(None, 'feat')
All inputs are finite; a program needn't handle non-finite values.
Results may differ from a plain program's by a relative error of at most 0.001.
The roundings to bfloat16 on the way count: a program that leaves them out, or rounds other values in their place, can miss the bound.
Values may be sent and summed in bfloat16 or wider, within the bound.
A program may use at most 128 MiB of HBM per device.

v0:
```python
import math

import jax
import jax.numpy as jnp
from jax import lax
from jax.sharding import PartitionSpec as P

F = 2048
ITERS = 3


ridge = 0.05
contract_last = (((1,), (1,)), ((), ()))
contract_first = (((0,), (0,)), ((), ()))


def column_softmax(scores):
    column_max = jnp.max(scores, axis=0, keepdims=True)
    shifted_exp = jnp.exp(scores - column_max)
    return shifted_exp / jnp.sum(shifted_exp, axis=0, keepdims=True)


def total_one(amount):
    return lax.psum(amount, "feat")


def on_device(features, labels, weights, sketch_basis, sketch_values):
    classes, local_cols = weights.shape
    local_rows = features.shape[0]
    sketch_rank = sketch_basis.shape[2]
    samp_count = lax.axis_size("samp")
    total_rows = local_rows * samp_count
    onehot = (labels[None, :] == jnp.arange(classes, dtype=jnp.int32)[:, None]).astype(jnp.float32)

    def class_logits(rounded):
        partial_logits = lax.dot_general(
            rounded, features, contract_last, preferred_element_type=jnp.float32
        )
        return lax.psum(partial_logits, "feat")

    def feature_sums(coeffs):
        coeffs_b = coeffs.astype(jnp.bfloat16)
        partial_cols = jnp.dot(coeffs_b, features, preferred_element_type=jnp.float32)
        return lax.psum(partial_cols, "samp")

    weights_b = weights.astype(jnp.bfloat16)
    probabilities = column_softmax(class_logits(weights_b) / math.sqrt(F))
    gradient = feature_sums(probabilities - onehot) * (math.sqrt(F) / total_rows) + ridge * weights
    flat_local = sketch_basis.reshape(classes * local_cols, sketch_rank)
    local_gram = lax.dot_general(
        flat_local, flat_local, contract_first, precision=lax.Precision.HIGHEST
    )
    gram_matrix = lax.psum(local_gram, "feat")
    factor = jnp.linalg.cholesky(gram_matrix)
    coefficients = (jnp.min(sketch_values) + ridge) / (sketch_values + ridge) - 1.0
    basis_own = sketch_basis.reshape(classes * local_cols, sketch_rank)

    def precondition(residue):
        local_proj = jnp.dot(residue.reshape(-1), basis_own, precision=lax.Precision.HIGHEST)
        projection = total_one(local_proj)
        inner_coords = jax.scipy.linalg.solve_triangular(factor, projection, lower=True)
        weighted_coords = coefficients * inner_coords
        outer_coords = jax.scipy.linalg.solve_triangular(
            factor, weighted_coords, lower=True, trans=1
        )
        scaled_res = residue + jnp.dot(
            basis_own, outer_coords, precision=lax.Precision.HIGHEST
        ).reshape(residue.shape)
        return (scaled_res, total_one(jnp.sum(residue * scaled_res)))

    residue = -gradient
    newton_part = jnp.zeros_like(residue)
    scaled_res, res_dot = precondition(residue)
    direction = scaled_res
    for iteration in range(ITERS):
        hessian_rounded = direction.astype(jnp.bfloat16)
        image_vals = class_logits(hessian_rounded)
        weighted = probabilities * image_vals
        curvature = weighted - probabilities * jnp.sum(weighted, axis=0, keepdims=True)
        hess_image = feature_sums(curvature) / total_rows + ridge * direction
        step_size = res_dot / total_one(jnp.sum(direction * hess_image))
        newton_part = newton_part + step_size * direction
        if iteration + 1 < ITERS:
            residue = residue - step_size * hess_image
            scaled_res, new_dot = precondition(residue)
            direction = scaled_res + new_dot / res_dot * direction
            res_dot = new_dot
    return newton_part


def solution(mesh):
    in_specs = (P("samp", "feat"), P("samp"), P(None, "feat"), P(None, "feat", None), P())
    out_specs = P(None, "feat")
    return jax.shard_map(
        on_device, mesh=mesh, in_specs=in_specs, out_specs=out_specs, check_vma=False
    )
```

profile of v0, /device:TPU:0, one launch (start us, length us, event | category | flops | bytes accessed | tf_op | source)
XLA Modules:
  0.0 683.6 jit_solution(9069180844210770004)
XLA Ops:
  6.5 21.0 %convolution_bitcast_fusion = f32[512,512]{0,1:T(8,128)} fusion(f32[10,512,512]{2,1,0:T(8,128)} %param.12), kind=kOutput, calls=%fused_computation.2 | convolution fusion | flops 16106127360 | bytes 11534336 | tf_op jit(solution)/shard_map/dot_general | solution.py:50
  27.5 11.3 %fusion.94 = f32[10,16384]{1,0:T(8,128)} fusion(bf16[16384,512]{1,0:T(8,128)(2,1)} %param.9, f32[10,512]{1,0:T(8,128)S(1)} %copy-done.2), kind=kOutput, calls=%fused_computation.180 | convolution fusion | flops 167777280 | bytes 17453056 | tf_op jit(solution)/shard_map/dot_general | solution.py:36
  39.0 0.6 reduce_min.9
  40.3 52.8 %all-reduce.14.cloned.1.call-done = (f32[10,16384]{1,0:T(8,128)}, f32[512,512]{0,1:T(8,128)}) async-done(((f32[10,16384]{1,0:T(8,128)}, f32[512,512]{0,1:T(8,128)}), (f32[10,16384]{1,0:T(8,128)}, f32[512,512]{0,1:T(8,128)})) %all-reduce.14.cloned.1.call-update) | async-done | bytes 1703952 | tf_op jit(solution)/shard_map/psum | solution.py:39
  93.1 1.6 copy.8
  94.7 1.4 fusion.36
  96.2 11.7 %cholesky.104 = f32[128,128]{1,0:T(8,128)S(1)} custom-call(f32[128,128]{1,0:T(8,128)S(1)} %cholesky.266), custom_call_target="Cholesky" | custom-call | tf_op jit(solution)/shard_map/jit(cholesky)/cholesky | solution.py:54
  107.9 9.8 %custom-call.33 = f32[1,128,128]{1,2,0:T(8,128)S(1)} custom-call(f32[1,128,128]{2,1,0:T(8,128)S(1)} %get-tuple-element.78), custom_call_target="InvertDiagBlocksLowerTriangular" | custom-call | tf_op jit(solution)/shard_map/jit(cholesky)/cholesky | solution.py:54
  118.5 11.7 %cholesky.217 = f32[128,128]{1,0:T(8,128)S(1)} custom-call(f32[128,128]{1,0:T(8,128)S(1)} %cholesky.270), custom_call_target="Cholesky" | custom-call | tf_op jit(solution)/shard_map/jit(cholesky)/cholesky | solution.py:54
  130.3 10.0 %custom-call.34 = f32[1,128,128]{1,2,0:T(8,128)S(1)} custom-call(f32[1,128,128]{2,1,0:T(8,128)S(1)} %get-tuple-element.75), custom_call_target="InvertDiagBlocksLowerTriangular" | custom-call | tf_op jit(solution)/shard_map/jit(cholesky)/cholesky | solution.py:54
  140.9 11.7 %cholesky.238 = f32[128,128]{1,0:T(8,128)S(1)} custom-call(f32[128,128]{1,0:T(8,128)S(1)} %cholesky.275), custom_call_target="Cholesky" | custom-call | tf_op jit(solution)/shard_map/jit(cholesky)/cholesky | solution.py:54
  152.7 0.7 compare_reduce_fusion.1
  153.4 9.8 %custom-call.35 = f32[1,128,128]{1,2,0:T(8,128)S(1)} custom-call(f32[1,128,128]{2,1,0:T(8,128)S(1)} %get-tuple-element.72), custom_call_target="InvertDiagBlocksLowerTriangular" | custom-call | tf_op jit(solution)/shard_map/jit(cholesky)/cholesky | solution.py:54
  163.8 11.7 %cholesky.255 = f32[128,128]{1,0:T(8,128)S(1)} custom-call(f32[128,128]{1,0:T(8,128)S(1)} %convolution_subtract_fusion.2), custom_call_target="Cholesky" | custom-call | tf_op jit(solution)/shard_map/jit(cholesky)/cholesky | solution.py:54
  175.6 0.6 compare_reduce_fusion
  176.2 0.7 compare_reduce_fusion.2
  180.0 8.1 %while.12 = (s32[]{:T(128)}, f32[512,512]{1,0:T(8,128)S(1)}, s32[4,2]{0,1:T(2,128)S(1)}, f32[4,128,128]{2,1,0:T(8,128)S(1)}, s32[]{:T(128)}) while((s32[]{:T(128)}, f32[512,512]{1,0:T(8,128)S(1)}, s32[4,2]{0,1:T(2,128)S(1)}, f32[4,128,128]{2,1,0:T(8,128)S(1)}, s32[]{:T(128)}) %tuple.47), condition=%wide.while_cond.1, body=%wide.while_body.1.sunk | while | flops 2 | bytes 131181 | solution.py:63
  180.1 0.6 fusion.251
  180.7 1.3 bitcast_dynamic-update-slice_fusion.2
  182.1 0.6 fusion.251
  182.7 1.3 bitcast_dynamic-update-slice_fusion.2
  184.1 0.6 fusion.251
  184.7 1.3 bitcast_dynamic-update-slice_fusion.2
  186.8 1.3 bitcast_dynamic-update-slice_fusion.2
  188.1 39.3 %custom-call.41 = f32[4,128,128]{1,2,0:T(8,128)S(1)} custom-call(f32[4,128,128]{2,1,0:T(8,128)S(1)} %get-tuple-element.48), custom_call_target="InvertDiagBlocksLowerTriangular" | custom-call | tf_op jit(solution)/shard_map/jit(_solve_triangular)/triangular_solve | solution.py:63
  227.4 1.5 multiply_reduce_fusion
  228.9 1.5 fusion.38
  230.4 8.4 %fusion.39 = f32[10,512]{1,0:T(8,128)S(1)} fusion(bf16[16384,512]{1,0:T(8,128)(2,1)} %param.9, s32[16384]{0:T(1024)S(1)} %copy-done.1, f32[10,16384]{1,0:T(8,128)} %get-tuple-element.65, f32[16384]{0:T(1024)S(1)} %fusion.38, f32[16384]{0:T(1024)S(1)} %multiply_reduce_fusion), kind=kOutput, calls=%fused_computation.99 | convolution fusion | flops 168919040 | bytes 17649664 | tf_op jit(solution)/shard_map/dot_general | solution.py:43
  238.8 37.1 %psum.127 = f32[10,512]{1,0:T(8,128)S(1)} all-reduce(f32[10,512]{1,0:T(8,128)S(1)} %fusion.39), channel_id=1, replica_groups=mesh['samp'=8,'feat'=4] {'samp'}, use_global_device_ids=true, to_apply=%region_3.0 | all-reduce | flops 5120 | bytes 40960 | tf_op jit(solution)/shard_map/psum | solution.py:44
  275.9 7.6 %fusion.86 = f32[1,512,1]{1,0,2:T(1,128)S(1)} fusion(f32[10,512,512]{2,1,0:T(8,128)} %param.12, f32[10,512,1]{1,0,2:T(8,128)S(1)} %bitcast.442), kind=kOutput, calls=%fused_computation.172 | convolution fusion | flops 31457280 | bytes 10508288 | tf_op jit(solution)/shard_map/dot_general | solution.py:59
  283.5 6.0 psum.129
  292.4 11.2 %fusion.96 = f32[1,10,512]{2,0,1:T(1,128)S(1)} fusion(f32[10,512,512]{2,1,0:T(8,128)} %param.12, f32[128,1]{0,1:T(1,128)S(1)} %convolution_bitcast_fusion.30, f32[128,1]{0,1:T(1,128)S(1)} %convolution_bitcast_fusion.28, f32[128,1]{0,1:T(1,128)S(1)} %convolution_bitcast_fusion.26, f32[128,1]{0,1:T(1,128)S(1)} %convolution_bitcast_fusion.25), kind=kOutput, calls=%fused_computation.184 | convolution fusion | flops 31458816 | bytes 10508288 | tf_op jit(solution)/shard_map/dot_general | solution.py:66
  303.6 11.2 %fusion.92 = f32[10,16384]{1,0:T(8,128)} fusion(bf16[16384,512]{1,0:T(8,128)(2,1)} %param.9, f32[10,512]{1,0:T(8,128)S(1)} %add_negate_fusion, f32[1,10,512]{2,0,1:T(1,128)S(1)} %fusion.96), kind=kOutput, calls=%fused_computation.178 | convolution fusion | flops 167782400 | bytes 17473536 | tf_op jit(solution)/shard_map/dot_general | solution.py:36
  314.9 32.8 %all-reduce.8.cloned.1.call-done = f32[10,16384]{1,0:T(8,128)} async-done(((f32[10,16384]{1,0:T(8,128)}), f32[10,16384]{1,0:T(8,128)}) %all-reduce.8.cloned.1.call-update) | async-done | bytes 655376 | tf_op jit(solution)/shard_map/psum | solution.py:39
  347.8 1.6 fusion.203
  349.4 8.4 %fusion.40 = f32[10,512]{1,0:T(8,128)S(1)} fusion(bf16[16384,512]{1,0:T(8,128)(2,1)} %param.9, f32[16384]{0:T(1024)S(1)} %fusion.203, f32[10,16384]{1,0:T(8,128)S(1)} %copy-done, f32[16384]{0:T(1024)S(1)} %fusion.38, f32[16384]{0:T(1024)S(1)} %multiply_reduce_fusion, f32[10,16384]{1,0:T(8,128)} %all-reduce.8.cloned.1.call-done), kind=kOutput, calls=%fused_computation.100 | convolution fusion | flops 168919040 | bytes 18305024 | tf_op jit(solution)/shard_map/dot_general | solution.py:43
  357.8 37.1 %psum.132 = f32[10,512]{1,0:T(8,128)S(1)} all-reduce(f32[10,512]{1,0:T(8,128)S(1)} %fusion.40), channel_id=1, replica_groups=mesh['samp'=8,'feat'=4] {'samp'}, use_global_device_ids=true, to_apply=%region_19.22 | all-reduce | flops 5120 | bytes 40960 | tf_op jit(solution)/shard_map/psum | solution.py:44
  394.8 0.7 multiply_reduce_fusion.3
  395.5 6.3 all-reduce.1
  403.1 7.6 %fusion.84 = f32[1,512,1]{1,0,2:T(1,128)S(1)} fusion(f32[10,512,512]{2,1,0:T(8,128)} %param.12, f32[10,512,1]{1,0,2:T(8,128)S(1)} %bitcast.443), kind=kOutput, calls=%fused_computation.170 | convolution fusion | flops 31457280 | bytes 10508288 | tf_op jit(solution)/shard_map/dot_general | solution.py:59
  410.7 6.6 psum.134
  420.3 11.2 %fusion.103 = f32[1,10,512]{2,0,1:T(1,128)S(1)} fusion(f32[10,512,512]{2,1,0:T(8,128)} %param.12, f32[128,1]{0,1:T(1,128)S(1)} %convolution_bitcast_fusion.18, f32[128,1]{0,1:T(1,128)S(1)} %convolution_bitcast_fusion.16, f32[128,1]{0,1:T(1,128)S(1)} %convolution_bitcast_fusion.14, f32[128,1]{0,1:T(1,128)S(1)} %convolution_bitcast_fusion.13), kind=kOutput, calls=%fused_computation.193 | convolution fusion | flops 31458816 | bytes 10508288 | tf_op jit(solution)/shard_map/dot_general | solution.py:66
  431.5 0.6 fusion.81
  432.1 6.3 psum.135
  439.6 11.3 %fusion.90 = f32[10,16384]{1,0:T(8,128)} fusion(bf16[16384,512]{1,0:T(8,128)(2,1)} %param.9, f32[10,512]{1,0:T(8,128)S(1)} %fusion.79), kind=kOutput, calls=%fused_computation.176 | convolution fusion | flops 167777280 | bytes 17453056 | tf_op jit(solution)/shard_map/dot_general | solution.py:36
  451.0 33.1 %all-reduce.10.cloned.1.call-done = f32[10,16384]{1,0:T(8,128)} async-done(((f32[10,16384]{1,0:T(8,128)}), f32[10,16384]{1,0:T(8,128)}) %all-reduce.10.cloned.1.call-update) | async-done | bytes 655376 | tf_op jit(solution)/shard_map/psum | solution.py:39
  484.1 1.6 fusion.205
  485.7 8.4 %fusion.41 = f32[10,512]{1,0:T(8,128)S(1)} fusion(bf16[16384,512]{1,0:T(8,128)(2,1)} %param.9, f32[16384]{0:T(1024)S(1)} %fusion.205, f32[10,16384]{1,0:T(8,128)S(1)} %copy-done, f32[16384]{0:T(1024)S(1)} %fusion.38, f32[16384]{0:T(1024)S(1)} %multiply_reduce_fusion, f32[10,16384]{1,0:T(8,128)} %all-reduce.10.cloned.1.call-done), kind=kOutput, calls=%fused_computation.101 | convolution fusion | flops 168919040 | bytes 18305024 | tf_op jit(solution)/shard_map/dot_general | solution.py:43
  494.1 37.1 %psum.137 = f32[10,512]{1,0:T(8,128)S(1)} all-reduce(f32[10,512]{1,0:T(8,128)S(1)} %fusion.41), channel_id=1, replica_groups=mesh['samp'=8,'feat'=4] {'samp'}, use_global_device_ids=true, to_apply=%region_27.30 | all-reduce | flops 5120 | bytes 40960 | tf_op jit(solution)/shard_map/psum | solution.py:44
  531.2 0.7 multiply_reduce_fusion.2
  531.9 6.3 psum.138
  539.6 7.6 %fusion.82 = f32[1,512,1]{1,0,2:T(1,128)S(1)} fusion(f32[10,512,512]{2,1,0:T(8,128)} %param.12, f32[10,512,1]{1,0,2:T(8,128)S(1)} %bitcast.444), kind=kOutput, calls=%fused_computation.168 | convolution fusion | flops 31457280 | bytes 10508288 | tf_op jit(solution)/shard_map/dot_general | solution.py:59
  547.3 6.7 psum.139
  556.8 11.2 %fusion.110 = f32[1,10,512]{2,0,1:T(1,128)S(1)} fusion(f32[10,512,512]{2,1,0:T(8,128)} %param.12, f32[128,1]{0,1:T(1,128)S(1)} %convolution_bitcast_fusion.6, f32[128,1]{0,1:T(1,128)S(1)} %convolution_bitcast_fusion.4, f32[128,1]{0,1:T(1,128)S(1)} %convolution_bitcast_fusion.2, f32[128,1]{0,1:T(1,128)S(1)} %convolution_bitcast_fusion.1), kind=kOutput, calls=%fused_computation.202 | convolution fusion | flops 31458816 | bytes 10508288 | tf_op jit(solution)/shard_map/dot_general | solution.py:66
  568.0 0.6 fusion.78
  568.7 6.3 psum.140
  576.3 11.3 %fusion.88 = f32[10,16384]{1,0:T(8,128)} fusion(bf16[16384,512]{1,0:T(8,128)(2,1)} %param.9, f32[10,512]{1,0:T(8,128)S(1)} %fusion.76), kind=kOutput, calls=%fused_computation.174 | convolution fusion | flops 167777280 | bytes 17453056 | tf_op jit(solution)/shard_map/dot_general | solution.py:36
  587.6 33.2 %all-reduce.12.cloned.1.call-done = f32[10,16384]{1,0:T(8,128)} async-done(((f32[10,16384]{1,0:T(8,128)}), f32[10,16384]{1,0:T(8,128)}) %all-reduce.12.cloned.1.call-update) | async-done | bytes 655376 | tf_op jit(solution)/shard_map/psum | solution.py:39
  620.8 1.6 fusion.207
  622.4 8.4 %fusion.42 = f32[10,512]{1,0:T(8,128)S(1)} fusion(bf16[16384,512]{1,0:T(8,128)(2,1)} %param.9, f32[16384]{0:T(1024)S(1)} %fusion.207, f32[10,16384]{1,0:T(8,128)S(1)} %copy-done, f32[16384]{0:T(1024)S(1)} %fusion.38, f32[16384]{0:T(1024)S(1)} %multiply_reduce_fusion, f32[10,16384]{1,0:T(8,128)} %all-reduce.12.cloned.1.call-done), kind=kOutput, calls=%fused_computation.102 | convolution fusion | flops 168919040 | bytes 18305024 | tf_op jit(solution)/shard_map/dot_general | solution.py:43
  630.8 37.1 %psum.142 = f32[10,512]{1,0:T(8,128)S(1)} all-reduce(f32[10,512]{1,0:T(8,128)S(1)} %fusion.42), channel_id=1, replica_groups=mesh['samp'=8,'feat'=4] {'samp'}, use_global_device_ids=true, to_apply=%region_35.38 | all-reduce | flops 5120 | bytes 40960 | tf_op jit(solution)/shard_map/psum | solution.py:44
  667.8 0.6 multiply_reduce_fusion.1
  668.5 6.3 psum.143
  676.0 0.6 multiply_add_fusion
  (92 shorter events, 12.8 us)
Async XLA Ops:
  6.5 21.0 %copy-start.2 = (f32[10,512]{1,0:T(8,128)S(1)}, f32[10,512]{1,0:T(8,128)}, u32[]{:S(2)}) copy-start(f32[10,512]{1,0:T(8,128)} %param.11) | copy-start | bytes 61444
  6.5 86.6 %all-reduce.14.cloned.1.call-start = ((), (), s32[]{:S(2)}) async-start(), calls=%async_computation.3 | async-start | bytes 4194304 | tf_op jit(solution)/shard_map/psum | solution.py:39
  27.5 11.5 %copy-start.3 = (f32[512]{0:T(512)S(1)}, f32[512]{0:T(512)}, u32[]{:S(2)}) copy-start(f32[512]{0:T(512)} %param.13) | copy-start | bytes 6148
  27.5 202.9 %copy-start.1 = (s32[16384]{0:T(1024)S(1)}, s32[16384]{0:T(1024)}, u32[]{:S(2)}) copy-start(s32[16384]{0:T(1024)} %param.10) | copy-start | bytes 196612
  38.8 309.0 %all-reduce.8.cloned.1.call-start = ((), (), s32[]{:S(2)}) async-start(), calls=%async_computation | async-start | bytes 2097152 | tf_op jit(solution)/shard_map/psum | solution.py:39
  283.5 64.2 %copy-start = (f32[10,16384]{1,0:T(8,128)S(1)}, f32[10,16384]{1,0:T(8,128)}, u32[]{:S(2)}) copy-start(f32[10,16384]{1,0:T(8,128)} %get-tuple-element.65) | copy-start | bytes 1966084
  314.9 169.2 %all-reduce.10.cloned.1.call-start = ((), (), s32[]{:S(2)}) async-start(), calls=%async_computation.1 | async-start | bytes 2097152 | tf_op jit(solution)/shard_map/psum | solution.py:39
  450.9 169.8 %all-reduce.12.cloned.1.call-start = ((), (), s32[]{:S(2)}) async-start(), calls=%async_computation.2 | async-start | bytes 2097152 | tf_op jit(solution)/shard_map/psum | solution.py:39
Sparse Core Ops, SparseCore 0:
  38.9 54.1 all-reduce.13
  315.0 32.7 all-reduce.7
  451.1 33.0 all-reduce.9
  587.7 33.0 all-reduce.11
where the time goes:
time: 690 us; the launch traced here: 684 us
  blocking collectives  199 us (29%)
  matrix products  167 us (24%)
  waiting for transfers between devices  152 us (22%)
  other arithmetic  132 us (19%)
  between operations  23.5 us (3%)
  local copies, waits for them, and re-layouts  9.76 us (1%)
    psum x4, waiting for transfers between devices, class_logits(): return lax.psum(partial_logits, 'feat')  152 us
    psum x4, blocking collectives, feature_sums(): return lax.psum(partial_cols, 'samp')  148 us
    another operation x14, other arithmetic, on_device(): factor = jnp.linalg.cholesky(gram_matrix)  78.7 us
    psum x8, blocking collectives, total_one(): return lax.psum(amount, 'feat')  50.6 us
    dot_general x4, matrix products, class_logits(): lax.dot_general(rounded, features, contract_last, preferred_element_type=...  45.1 us
    another operation x4, other arithmetic, precondition(): jax.scipy.linalg.solve_triangular(factor, weighted_coords, lower=True, tr...  39.8 us
    dot_general x3, matrix products, precondition(): jnp.dot(basis_own, outer_coords, precision=lax.Precision.HIGHEST)  33.6 us
    dot_general x4, matrix products, feature_sums(): jnp.dot(coeffs_b, features, preferred_element_type=jnp.float32)  33.5 us
  transfers between devices with their start and end apart: 4, of which 4 were waited for; matrix products, arithmetic and copies ran while one was open for 0% of the time, Pallas kernels for 0%

commit v1 on v0

v1 whole, which is shorter than its diff:
```python
import functools
import math

import jax
import jax.numpy as jnp
from jax import lax
from jax.experimental import pallas as pl
from jax.experimental.pallas import tpu as pltpu
from jax.sharding import PartitionSpec as P

ITERS = 3


ridge = 0.05
contract_last = (((1,), (1,)), ((), ()))
contract_first = (((0,), (0,)), ((), ()))
MESH = pl.DeviceIdType.MESH
HIGHEST = lax.Precision.HIGHEST


def column_softmax(scores):
    column_max = jnp.max(scores, axis=0, keepdims=True)
    shifted_exp = jnp.exp(scores - column_max)
    return shifted_exp / jnp.sum(shifted_exp, axis=0, keepdims=True)


def product_kernel(first, nf, ns, scale, tile, *refs):
    if first:
        (feat_ref, vec_ref, lab_ref, out_ref, prob_ref,
         fbuf, part, got, coef, sums, load_sem,
         s1, r1, s2, r2, s3, r3) = refs
    else:
        (feat_ref, vec_ref, prob_ref, out_ref,
         fbuf, part, got, coef, sums, load_sem,
         s1, r1, s2, r2, s3, r3) = refs
    me = lax.axis_index("feat")
    row = lax.axis_index("samp")
    classes = vec_ref.shape[0]
    share = fbuf.shape[1]
    order = sorted(range(1, nf), key=lambda s: -min(s, nf - s)) + [0]

    loads = {}
    for s in order:
        q = lax.rem(me + s, nf)
        loads[s] = pltpu.make_async_copy(
            feat_ref.at[pl.ds(pl.multiple_of(q * share, share), share), :],
            fbuf.at[s], load_sem.at[s])
        loads[s].start()
    barrier = pltpu.get_barrier_semaphore()
    for s in range(1, nf):
        pl.semaphore_signal(barrier, inc=1, device_id={"feat": lax.rem(me + s, nf)}, device_id_type=MESH)
    for s in range(1, ns):
        pl.semaphore_signal(barrier, inc=1, device_id={"samp": lax.rem(row + s, ns)}, device_id_type=MESH)

    vec = vec_ref[...]
    sends = []
    for at, s in enumerate(order):
        loads[s].wait()

        @pl.loop(0, share // tile)
        def _(i, s=s):
            rows = pl.ds(pl.multiple_of(i * tile, tile), tile)
            part[s, :, rows] = lax.dot_general(
                vec, fbuf[s, rows, :], contract_last, preferred_element_type=jnp.float32)
        if at == 0:
            pl.semaphore_wait(barrier, nf - 1 + ns - 1)
        if s:
            copy = pltpu.make_async_remote_copy(
                src_ref=part.at[s], dst_ref=got.at[s - 1],
                send_sem=s1.at[s - 1], recv_sem=r1.at[s - 1],
                device_id={"feat": lax.rem(me + s, nf)}, device_id_type=MESH)
            copy.start()
            sends.append(copy)
    for copy in sends:
        copy.wait_recv()

    @pl.loop(0, share // tile)
    def _(i):
        rows = pl.ds(pl.multiple_of(i * tile, tile), tile)
        scores = part[0, :, rows]
        for s in range(nf - 1):
            scores = scores + got[s, :, rows]
        if first:
            prob = column_softmax(scores * scale)
            prob_ref[:, rows] = prob
            hot = lab_ref[:, rows] == lax.broadcasted_iota(jnp.int32, (classes, tile), 0)
            coef[0, :, rows] = (prob - hot.astype(jnp.float32)).astype(jnp.bfloat16)
        else:
            prob = prob_ref[:, rows]
            weighted = prob * scores
            coef[0, :, rows] = (
                weighted - prob * jnp.sum(weighted, axis=0, keepdims=True)).astype(jnp.bfloat16)

    gathers = {}
    for s in order[:-1]:
        copy = pltpu.make_async_remote_copy(
            src_ref=coef.at[0], dst_ref=coef.at[nf - s],
            send_sem=s2.at[s - 1], recv_sem=r2.at[nf - s - 1],
            device_id={"feat": lax.rem(me + s, nf)}, device_id_type=MESH)
        copy.start()
        gathers[s] = copy
    near = [s for s in reversed(order)]
    sums[0] = jnp.zeros(sums.shape[1:], jnp.float32)
    for s in near:
        if s:
            gathers[nf - s].wait_recv()

        @pl.loop(0, share // tile)
        def _(i, s=s):
            rows = pl.ds(pl.multiple_of(i * tile, tile), tile)
            sums[0] += jnp.dot(coef[s, :, rows], fbuf[s, rows, :], preferred_element_type=jnp.float32)
    totals = []
    for s in sorted(range(1, ns), key=lambda s: -min(s, ns - s)):
        copy = pltpu.make_async_remote_copy(
            src_ref=sums.at[0], dst_ref=sums.at[s],
            send_sem=s3.at[s - 1], recv_sem=r3.at[s - 1],
            device_id={"samp": lax.rem(row + s, ns)}, device_id_type=MESH)
        copy.start()
        totals.append(copy)
    for copy in totals:
        copy.wait_recv()
    total = sums[lax.rem(row, ns)]
    for t in range(1, ns):
        total = total + sums[lax.rem(row + ns - t, ns)]
    out_ref[...] = total
    for copy in sends + list(gathers.values()) + totals:
        copy.wait_send()


def sample_product(first, features, vector, side, nf, ns, scale):
    classes, cols = vector.shape
    local_rows = features.shape[0]
    share = local_rows // nf
    tile = min(1024, share)
    out_shape = [jax.ShapeDtypeStruct((classes, cols), jnp.float32)]
    if first:
        out_shape.append(jax.ShapeDtypeStruct((classes, share), jnp.float32))
    vmem = pl.BlockSpec(memory_space=pltpu.VMEM)
    dma = pltpu.SemaphoreType.DMA
    return pl.pallas_call(
        functools.partial(product_kernel, first, nf, ns, scale, tile),
        out_shape=out_shape,
        in_specs=[pl.BlockSpec(memory_space=pl.ANY), vmem, vmem],
        out_specs=[vmem] * len(out_shape),
        scratch_shapes=[
            pltpu.VMEM((nf, share, cols), jnp.bfloat16),
            pltpu.VMEM((nf, classes, share), jnp.float32),
            pltpu.VMEM((nf - 1, classes, share), jnp.float32),
            pltpu.VMEM((nf, classes, share), jnp.bfloat16),
            pltpu.VMEM((ns, classes, cols), jnp.float32),
            dma((nf,)),
            dma((nf - 1,)), dma((nf - 1,)),
            dma((nf - 1,)), dma((nf - 1,)),
            dma((ns - 1,)), dma((ns - 1,)),
        ],
        compiler_params=pltpu.CompilerParams(
            collective_id=0 if first else 1, has_side_effects=True,
            vmem_limit_bytes=48 * 1024 * 1024),
        cost_estimate=pl.CostEstimate(
            flops=4 * classes * local_rows * cols, bytes_accessed=2 * local_rows * cols, transcendentals=0),
        name="first_product" if first else "curvature_product",
    )(features, vector, side)


def on_device(features, labels, weights, sketch_basis, sketch_values):
    classes, local_cols = weights.shape
    local_rows = features.shape[0]
    sketch_rank = sketch_basis.shape[2]
    ns, nf = lax.axis_size("samp"), lax.axis_size("feat")
    total_rows = local_rows * ns
    total_cols = local_cols * nf
    share = local_rows // nf

    flat_local = sketch_basis.reshape(classes * local_cols, sketch_rank)
    local_gram = lax.dot_general(flat_local, flat_local, contract_first, precision=HIGHEST)
    gram_matrix = lax.psum(local_gram, "feat")

    own_labels = lax.dynamic_slice(labels, (lax.axis_index("feat") * share,), (share,))[None, :]
    sums, probabilities = sample_product(
        True, features, weights.astype(jnp.bfloat16), own_labels, nf, ns, 1.0 / math.sqrt(total_cols))
    gradient = sums * (math.sqrt(total_cols) / total_rows) + ridge * weights

    factor = jnp.linalg.cholesky(gram_matrix)
    coefficients = (jnp.min(sketch_values) + ridge) / (sketch_values + ridge) - 1.0
    inverse = jax.scipy.linalg.solve_triangular(
        factor, jnp.eye(sketch_rank, dtype=jnp.float32), lower=True)

    def precondition(residue):
        local_proj = jnp.dot(residue.reshape(-1), flat_local, precision=HIGHEST)
        both = lax.psum(jnp.concatenate([local_proj, jnp.sum(residue * residue)[None]]), "feat")
        inner = jnp.sum(inverse * both[None, :sketch_rank], axis=1)
        outer = jnp.sum(inverse * (coefficients * inner)[:, None], axis=0)
        scaled = residue + jnp.dot(flat_local, outer, precision=HIGHEST).reshape(residue.shape)
        return scaled, both[sketch_rank] + jnp.sum(coefficients * inner * inner)

    residue = -gradient
    newton_part = jnp.zeros_like(residue)
    scaled_res, res_dot = precondition(residue)
    direction = scaled_res
    for iteration in range(ITERS):
        (sums,) = sample_product(
            False, features, direction.astype(jnp.bfloat16), probabilities, nf, ns, 1.0)
        hess_image = sums / total_rows + ridge * direction
        step_size = res_dot / lax.psum(jnp.sum(direction * hess_image), "feat")
        newton_part = newton_part + step_size * direction
        if iteration + 1 < ITERS:
            residue = residue - step_size * hess_image
            scaled_res, new_dot = precondition(residue)
            direction = scaled_res + new_dot / res_dot * direction
            res_dot = new_dot
    return newton_part


def solution(mesh):
    in_specs = (P("samp", "feat"), P("samp"), P(None, "feat"), P(None, "feat", None), P())
    out_specs = P(None, "feat")
    return jax.shard_map(
        on_device, mesh=mesh, in_specs=in_specs, out_specs=out_specs, check_vma=False
    )
```

time: 690 us -> 454 us (0.66)
  blocking collectives: 199 us -> 39.3 us
  waiting for transfers between devices: 152 us -> 0.04 us
  Pallas kernels: 0 us -> 143 us
  matrix products: 167 us -> 87.4 us
    psum x12 -> x6, blocking collectives: 199 us -> 39.3 us  [the longest x3 19.8 us: precondition(): lax.psum(jnp.concatenate([local_proj, jnp.sum(residue * residue)[None]]),...]
    psum x4 -> x1, waiting for transfers between devices: 152 us -> 0.02 us  [on_device(): gram_matrix = lax.psum(local_gram, 'feat')]
    pallas_call x0 -> x4, Pallas kernels: none -> 143 us  [sample_product(): pl.pallas_call(functools.partial(product_kernel, first, nf, ns, scale, ti...]
    dot_general x15 -> x7, matrix products: 156 us -> 77.4 us  [the longest x3 33.5 us: precondition(): jnp.dot(flat_local, outer, precision=HIGHEST).reshape(residue.shape)]
    another operation x7 -> x3, other arithmetic: 39.9 us -> 40.3 us  [on_device(): jax.scipy.linalg.solve_triangular(factor, jnp.eye(sketch_rank, dtype=jnp....]
  transfers between devices with their start and end apart: 4 -> 1, of which waited for: 4 -> 0; matrix products, arithmetic and copies ran while one was open for 0% -> 2% of each run, Pallas kernels for 0% -> 10%
where the time goes in v1:
time: 454 us; the launch traced here: 446 us
  Pallas kernels  143 us (31%)
  other arithmetic  137 us (30%)
  matrix products  87.4 us (19%)
  blocking collectives  39.3 us (9%)
  between operations  23.2 us (5%)
  local copies, waits for them, and re-layouts  16.5 us (4%)
    pallas_call x4, Pallas kernels, sample_product(): pl.pallas_call(functools.partial(product_kernel, first, nf, ns, scale, ti...  143 us
    another operation x14, other arithmetic, on_device(): factor = jnp.linalg.cholesky(gram_matrix)  84.1 us
    another operation x3, other arithmetic, on_device(): jax.scipy.linalg.solve_triangular(factor, jnp.eye(sketch_rank, dtype=jnp....  40.3 us
    dot_general x3, matrix products, precondition(): jnp.dot(flat_local, outer, precision=HIGHEST).reshape(residue.shape)  33.5 us
    dot_general x3, matrix products, precondition(): local_proj = jnp.dot(residue.reshape(-1), flat_local, precision=HIGHEST)  22.9 us
    dot_general x1, matrix products, on_device(): lax.dot_general(flat_local, flat_local, contract_first, precision=HIGHEST)  21 us
    psum x3, blocking collectives, precondition(): lax.psum(jnp.concatenate([local_proj, jnp.sum(residue * residue)[None]]),...  19.8 us
    psum x3, blocking collectives, on_device(): step_size = res_dot / lax.psum(jnp.sum(direction * hess_image), 'feat')  19.6 us
  transfers between devices with their start and end apart: 1, of which 0 were waited for; matrix products, arithmetic and copies ran while one was open for 2% of the time, Pallas kernels for 10%

profile of v1, /device:TPU:0, one launch (start us, length us, event | category | flops | bytes accessed | tf_op | source)
XLA Modules:
  0.0 446.4 jit_solution(2008724152267108236)
XLA Ops:
  6.5 21.0 %convolution_bitcast_fusion = f32[512,512]{0,1:T(8,128)} fusion(f32[10,512,512]{2,1,0:T(8,128)} %param.8), kind=kOutput, calls=%fused_computation.2 | convolution fusion | flops 16106127360 | bytes 11534336 | tf_op jit(solution)/shard_map/dot_general | solution.py:175
  27.6 0.7 dynamic_slice.3
  28.3 46.1 %first_product.1 = (f32[10,512]{1,0:T(8,128)S(1)}, f32[10,4096]{1,0:T(8,128)S(1)}) custom-call(bf16[16384,512]{1,0:T(8,128)(2,1)} %refs_0_.7, bf16[10,512]{1,0:T(8,128)(2,1)S(1)} %convert_element_type.19.refs_1_, s32[1,4096]{1,0:T(1,128)S(1)} %bitcast.102), custom_call_target="tpu_custom_call" | custom-call | flops 335544320 | bytes 16777216 | tf_op jit(solution)/shard_map/first_product/pallas_call | solution.py:140
  74.5 7.6 %fusion.35 = f32[1,512,1]{1,0,2:T(1,128)S(1)} fusion(f32[10,512,512]{2,1,0:T(8,128)} %param.8, f32[10,512,1]{1,0,2:T(8,128)S(1)} %get-tuple-element.39), kind=kOutput, calls=%fused_computation.86 | convolution fusion | flops 31457280 | bytes 10508288 | tf_op jit(solution)/shard_map/dot_general | solution.py:189
  82.1 0.6 multiply_reduce_fusion.11
  82.7 0.6 pad_maximum_fusion.1
  83.3 5.8 %psum.49 = f32[513]{0:T(1024)S(1)} all-reduce(f32[513]{0:T(1024)S(1)} %pad_maximum_fusion.1), channel_id=1, replica_groups=mesh['samp'=8,'feat'=4] {'feat'}, use_global_device_ids=true, to_apply=%region_1.2 | all-reduce | flops 513 | bytes 4104 | tf_op jit(solution)/shard_map/psum | solution.py:190
  89.2 0.6 reduce_min.9
  90.4 0.8 iota_compare_fusion
  91.4 1.6 copy.8
  92.9 1.4 fusion
  94.4 11.7 %cholesky.104 = f32[128,128]{1,0:T(8,128)S(1)} custom-call(f32[128,128]{1,0:T(8,128)S(1)} %cholesky.266), custom_call_target="Cholesky" | custom-call | tf_op jit(solution)/shard_map/jit(cholesky)/cholesky | solution.py:183
  106.2 10.4 %custom-call.31 = f32[1,128,128]{1,2,0:T(8,128)} custom-call(f32[1,128,128]{2,1,0:T(8,128)S(1)} %get-tuple-element.52), custom_call_target="InvertDiagBlocksLowerTriangular" | custom-call | tf_op jit(solution)/shard_map/jit(cholesky)/cholesky | solution.py:183
  116.7 1.2 constant_dynamic-update-slice_fusion.3
  118.2 0.7 copy-done
  118.9 0.6 cholesky.270
  119.5 12.5 %cholesky.217 = f32[128,128]{1,0:T(8,128)S(1)} custom-call(f32[128,128]{1,0:T(8,128)} %cholesky.270), custom_call_target="Cholesky" | custom-call | tf_op jit(solution)/shard_map/jit(cholesky)/cholesky | solution.py:183
  132.1 0.6 select_reduce_fusion.2
  132.7 10.8 %custom-call.32 = f32[1,128,128]{1,2,0:T(8,128)S(1)} custom-call(f32[1,128,128]{2,1,0:T(8,128)} %get-tuple-element.49), custom_call_target="InvertDiagBlocksLowerTriangular" | custom-call | tf_op jit(solution)/shard_map/jit(cholesky)/cholesky | solution.py:183
  143.5 1.2 convolution_dynamic-update-slice_fusion
  145.1 0.6 copy-done.1
  145.7 12.3 %cholesky.238 = f32[128,128]{1,0:T(8,128)} custom-call(f32[128,128]{1,0:T(8,128)S(1)} %cholesky.275), custom_call_target="Cholesky" | custom-call | tf_op jit(solution)/shard_map/jit(cholesky)/cholesky | solution.py:183
  158.1 0.9 select_reduce_fusion.1
  158.9 0.7 compare_reduce_fusion.1
  159.6 10.4 %custom-call.33 = f32[1,128,128]{1,2,0:T(8,128)} custom-call(f32[1,128,128]{2,1,0:T(8,128)S(1)} %get-tuple-element.46), custom_call_target="InvertDiagBlocksLowerTriangular" | custom-call | tf_op jit(solution)/shard_map/jit(cholesky)/cholesky | solution.py:183
  170.1 1.1 convolution_dynamic-update-slice_fusion.1
  171.5 11.7 %cholesky.255 = f32[128,128]{1,0:T(8,128)S(1)} custom-call(f32[128,128]{1,0:T(8,128)S(1)} %convolution_subtract_fusion.5), custom_call_target="Cholesky" | custom-call | tf_op jit(solution)/shard_map/jit(cholesky)/cholesky | solution.py:183
  183.7 0.7 compare_reduce_fusion
  184.4 0.7 compare_reduce_fusion.2
  187.7 10.6 %while.1 = (s32[]{:T(128)}, f32[512,512]{1,0:T(8,128)S(1)}, s32[4,2]{0,1:T(2,128)S(1)}, f32[4,128,128]{2,1,0:T(8,128)}, s32[]{:T(128)}) while((s32[]{:T(128)}, f32[512,512]{1,0:T(8,128)S(1)}, s32[4,2]{0,1:T(2,128)S(1)}, f32[4,128,128]{2,1,0:T(8,128)}, s32[]{:T(128)}) %tuple.35), condition=%wide.while_cond, body=%wide.while_body.sunk | while | flops 2 | bytes 132705 | solution.py:185
  187.8 0.6 fusion.71
  188.4 2.0 bitcast_dynamic-update-slice_fusion.2
  191.0 2.0 bitcast_dynamic-update-slice_fusion.2
  193.7 2.0 bitcast_dynamic-update-slice_fusion.2
  196.3 2.0 bitcast_dynamic-update-slice_fusion.2
  198.3 40.1 %custom-call.34 = f32[4,128,128]{1,2,0:T(8,128)S(1)} custom-call(f32[4,128,128]{2,1,0:T(8,128)} %get-tuple-element.16), custom_call_target="InvertDiagBlocksLowerTriangular" | custom-call | tf_op jit(solution)/shard_map/jit(_solve_triangular)/triangular_solve | solution.py:185
  238.4 1.2 fusion.11
  240.8 1.3 fusion.21
  242.1 0.6 convolution_subtract_fusion.2
  242.7 1.3 fusion.20
  244.2 0.6 multiply_reduce_fusion.14
  244.9 11.2 %fusion.51 = f32[1,10,512]{2,0,1:T(1,128)S(1)} fusion(f32[512,1,1]{0,1,2:T(1,128)S(1)} %bitcast.106, f32[10,512,512]{2,1,0:T(8,128)} %param.8), kind=kOutput, calls=%fused_computation.113 | convolution fusion | flops 31457280 | bytes 10508288 | tf_op jit(solution)/shard_map/dot_general | solution.py:193
  256.1 32.8 %curvature_product.3 = f32[10,512]{1,0:T(8,128)S(1)} custom-call(bf16[16384,512]{1,0:T(8,128)(2,1)} %refs_0_.7, bf16[10,512]{1,0:T(8,128)(2,1)S(1)} %fusion.42.refs_1_, f32[10,4096]{1,0:T(8,128)S(1)} %get-tuple-element.8.refs_2_), custom_call_target="tpu_custom_call" | custom-call | flops 335544320 | bytes 16777216 | tf_op jit(solution)/shard_map/curvature_product/pallas_call | solution.py:140
  288.9 0.6 multiply_reduce_fusion.10
  290.1 6.4 %psum.51 = f32[]{:T(128)} all-reduce(f32[]{:T(128)} %multiply_reduce_fusion.10), channel_id=1, replica_groups=mesh['samp'=8,'feat'=4] {'feat'}, use_global_device_ids=true, to_apply=%region_16.17 | all-reduce | flops 1 | bytes 8 | tf_op jit(solution)/shard_map/psum | solution.py:204
  298.5 0.6 multiply_reduce_fusion.9
  299.1 7.6 %fusion.33 = f32[1,512,1]{1,0,2:T(1,128)S(1)} fusion(f32[10,512,512]{2,1,0:T(8,128)} %param.8, f32[10,512,1]{1,0,2:T(8,128)S(1)} %bitcast.103), kind=kOutput, calls=%fused_computation.84 | convolution fusion | flops 31457280 | bytes 10508288 | tf_op jit(solution)/shard_map/dot_general | solution.py:189
  306.7 0.7 pad_maximum_fusion.2
  307.4 6.7 %psum.52 = f32[513]{0:T(1024)S(1)} all-reduce(f32[513]{0:T(1024)S(1)} %pad_maximum_fusion.2), channel_id=1, replica_groups=mesh['samp'=8,'feat'=4] {'feat'}, use_global_device_ids=true, to_apply=%region_18.19 | all-reduce | flops 513 | bytes 4104 | tf_op jit(solution)/shard_map/psum | solution.py:190
  314.8 0.7 multiply_reduce_fusion.13
  315.6 11.2 %fusion.52 = f32[1,10,512]{2,0,1:T(1,128)S(1)} fusion(f32[512,1,1]{0,1,2:T(1,128)S(1)} %bitcast.107, f32[10,512,512]{2,1,0:T(8,128)} %param.8), kind=kOutput, calls=%fused_computation.114 | convolution fusion | flops 31457280 | bytes 10508288 | tf_op jit(solution)/shard_map/dot_general | solution.py:193
  328.2 32.9 %curvature_product.4 = f32[10,512]{1,0:T(8,128)S(1)} custom-call(bf16[16384,512]{1,0:T(8,128)(2,1)} %refs_0_.7, bf16[10,512]{1,0:T(8,128)(2,1)S(1)} %get-tuple-element.31.refs_1_, f32[10,4096]{1,0:T(8,128)S(1)} %get-tuple-element.8.refs_2_), custom_call_target="tpu_custom_call" | custom-call | flops 335544320 | bytes 16777216 | tf_op jit(solution)/shard_map/curvature_product/pallas_call | solution.py:140
  361.1 0.6 multiply_reduce_fusion.8
  361.7 6.3 %psum.53 = f32[]{:T(128)} all-reduce(f32[]{:T(128)} %multiply_reduce_fusion.8), channel_id=1, replica_groups=mesh['samp'=8,'feat'=4] {'feat'}, use_global_device_ids=true, to_apply=%region_23.24 | all-reduce | flops 1 | bytes 8 | tf_op jit(solution)/shard_map/psum | solution.py:204
  368.7 0.6 multiply_reduce_fusion.7
  369.3 7.6 %fusion.31 = f32[1,512,1]{1,0,2:T(1,128)S(1)} fusion(f32[10,512,512]{2,1,0:T(8,128)} %param.8, f32[10,512,1]{1,0,2:T(8,128)S(1)} %bitcast.104), kind=kOutput, calls=%fused_computation.82 | convolution fusion | flops 31457280 | bytes 10508288 | tf_op jit(solution)/shard_map/dot_general | solution.py:189
  376.9 0.7 pad_maximum_fusion.3
  377.6 7.2 %psum.54 = f32[513]{0:T(1024)S(1)} all-reduce(f32[513]{0:T(1024)S(1)} %pad_maximum_fusion.3), channel_id=1, replica_groups=mesh['samp'=8,'feat'=4] {'feat'}, use_global_device_ids=true, to_apply=%region_25.26 | all-reduce | flops 513 | bytes 4104 | tf_op jit(solution)/shard_map/psum | solution.py:190
  385.5 0.7 multiply_reduce_fusion.12
  386.3 11.2 %fusion.53 = f32[1,10,512]{2,0,1:T(1,128)S(1)} fusion(f32[512,1,1]{0,1,2:T(1,128)S(1)} %bitcast.105, f32[10,512,512]{2,1,0:T(8,128)} %param.8), kind=kOutput, calls=%fused_computation.115 | convolution fusion | flops 31457280 | bytes 10508288 | tf_op jit(solution)/shard_map/dot_general | solution.py:193
  398.9 31.6 %curvature_product.5 = f32[10,512]{1,0:T(8,128)S(1)} custom-call(bf16[16384,512]{1,0:T(8,128)(2,1)} %refs_0_.7, bf16[10,512]{1,0:T(8,128)(2,1)S(1)} %get-tuple-element.25.refs_1_, f32[10,4096]{1,0:T(8,128)S(1)} %get-tuple-element.8.refs_2_), custom_call_target="tpu_custom_call" | custom-call | flops 335544320 | bytes 16777216 | tf_op jit(solution)/shard_map/curvature_product/pallas_call | solution.py:140
  430.5 0.6 multiply_reduce_fusion.6
  431.1 6.9 %psum.55 = f32[]{:T(128)} all-reduce(f32[]{:T(128)} %multiply_reduce_fusion.6), channel_id=1, replica_groups=mesh['samp'=8,'feat'=4] {'feat'}, use_global_device_ids=true, to_apply=%region_30.31 | all-reduce | flops 1 | bytes 8 | tf_op jit(solution)/shard_map/psum | solution.py:204
  438.7 0.6 multiply_add_fusion
  (51 shorter events, 7.9 us)
Async XLA Ops:
  6.5 21.1 %copy-start.3 = (f32[10,512]{1,0:T(8,128)S(1)}, f32[10,512]{1,0:T(8,128)}, u32[]{:S(2)}) copy-start(f32[10,512]{1,0:T(8,128)} %param.7) | copy-start | bytes 61444
  6.5 84.8 %all-reduce.3.cloned.1.call-start = ((), (), s32[]{:S(2)}) async-start(), calls=%async_computation | async-start | bytes 2097152 | tf_op jit(solution)/shard_map/psum | solution.py:176
  28.3 60.8 %copy-start.4 = (f32[512]{0:T(512)S(1)}, f32[512]{0:T(512)}, u32[]{:S(2)}) copy-start(f32[512]{0:T(512)} %param.9) | copy-start | bytes 6148
  118.2 0.7 copy-start
  145.1 0.6 copy-start.1
  238.4 1.6 copy-start.2
Sparse Core Ops, SparseCore 0:
  27.7 46.4 all-reduce.2

commit v2 on v1

--- a/solution.py
+++ b/solution.py
@@ -162,6 +162,60 @@
     )(features, vector, side)
 
 
+def inverse_factor_kernel(block, gram_ref, out_ref, work, low, tri):
+    size = gram_ref.shape[0]
+    rowid = lax.broadcasted_iota(jnp.int32, (block, block), 0)
+    lane = lax.broadcasted_iota(jnp.int32, (block, block), 1)
+    work[...] = gram_ref[...]
+    out_ref[...] = jnp.zeros_like(out_ref)
+    for at in range(0, size, block):
+        end = at + block
+        tri[...] = work[at:end, at:end]
+
+        @pl.loop(0, block)
+        def _(t):
+            held = tri[...]
+            row = tri[pl.ds(t, 1), :]
+            column = jnp.sum(jnp.where(lane == t, held, 0.0), axis=1, keepdims=True)
+            pivot = jnp.sum(jnp.where(lane[:1] == t, row, 0.0), axis=1, keepdims=True)
+            row = jnp.where(lane[:1] == t, 1.0, row) * (1.0 / pivot)
+            below = jnp.where(lane == t, 0.0, held) - column * row
+            tri[...] = jnp.where(rowid > t, below, held)
+
+        held = tri[...]
+        pivots = jnp.sum(jnp.where(lane == rowid, held, 0.0), axis=1, keepdims=True)
+        unit = jnp.where(lane < rowid, held, jnp.where(lane == rowid, 1.0, 0.0))
+        own = unit * (1.0 / jnp.sqrt(pivots))
+        out_ref[at:end, at:end] = own
+        if at:
+            inner = jnp.dot(low[at:end, :at], out_ref[:at, :at], precision=HIGHEST,
+                            preferred_element_type=jnp.float32)
+            out_ref[at:end, :at] = -jnp.dot(own, inner, precision=HIGHEST,
+                                            preferred_element_type=jnp.float32)
+        if end < size:
+            panel = lax.dot_general(work[end:, at:end], own, contract_last, precision=HIGHEST,
+                                    preferred_element_type=jnp.float32)
+            low[end:, at:end] = panel
+            work[end:, end:] -= lax.dot_general(panel, panel, contract_last, precision=HIGHEST,
+                                                preferred_element_type=jnp.float32)
+
+
+def inverse_factor(gram_matrix):
+    size = gram_matrix.shape[0]
+    block = math.gcd(size, 128)
+    vmem = pl.BlockSpec(memory_space=pltpu.VMEM)
+    return pl.pallas_call(
+        functools.partial(inverse_factor_kernel, block),
+        out_shape=jax.ShapeDtypeStruct((size, size), jnp.float32),
+        in_specs=[vmem],
+        out_specs=vmem,
+        scratch_shapes=[pltpu.VMEM((size, size), jnp.float32)] * 2 + [pltpu.VMEM((block, block), jnp.float32)],
+        compiler_params=pltpu.CompilerParams(vmem_limit_bytes=16 * 1024 * 1024),
+        cost_estimate=pl.CostEstimate(flops=12 * size ** 3, bytes_accessed=8 * size * size, transcendentals=0),
+        name="inverse_factor",
+    )(gram_matrix)
+
+
 def on_device(features, labels, weights, sketch_basis, sketch_values):
     classes, local_cols = weights.shape
     local_rows = features.shape[0]
@@ -172,7 +226,7 @@
     share = local_rows // nf
 
     flat_local = sketch_basis.reshape(classes * local_cols, sketch_rank)
-    local_gram = lax.dot_general(flat_local, flat_local, contract_first, precision=HIGHEST)
+    local_gram = lax.dot_general(flat_local, flat_local, contract_first, precision=lax.Precision.HIGH)
     gram_matrix = lax.psum(local_gram, "feat")
 
     own_labels = lax.dynamic_slice(labels, (lax.axis_index("feat") * share,), (share,))[None, :]
@@ -180,17 +234,15 @@
         True, features, weights.astype(jnp.bfloat16), own_labels, nf, ns, 1.0 / math.sqrt(total_cols))
     gradient = sums * (math.sqrt(total_cols) / total_rows) + ridge * weights
 
-    factor = jnp.linalg.cholesky(gram_matrix)
     coefficients = (jnp.min(sketch_values) + ridge) / (sketch_values + ridge) - 1.0
-    inverse = jax.scipy.linalg.solve_triangular(
-        factor, jnp.eye(sketch_rank, dtype=jnp.float32), lower=True)
+    inverse = inverse_factor(gram_matrix)
 
     def precondition(residue):
         local_proj = jnp.dot(residue.reshape(-1), flat_local, precision=HIGHEST)
         both = lax.psum(jnp.concatenate([local_proj, jnp.sum(residue * residue)[None]]), "feat")
         inner = jnp.sum(inverse * both[None, :sketch_rank], axis=1)
         outer = jnp.sum(inverse * (coefficients * inner)[:, None], axis=0)
-        scaled = residue + jnp.dot(flat_local, outer, precision=HIGHEST).reshape(residue.shape)
+        scaled = residue + jnp.sum(flat_local * outer[None, :], axis=1).reshape(residue.shape)
         return scaled, both[sketch_rank] + jnp.sum(coefficients * inner * inner)
 
     residue = -gradient

time: 454 us -> 323 us (0.71); the launches traced: 446 us -> 322 us
  other arithmetic: 137 us -> 24.1 us
  Pallas kernels: 143 us -> 198 us
  matrix products: 87.4 us -> 36.5 us
  local copies, waits for them, and re-layouts: 16.5 us -> 3.58 us
    another operation x17 -> x0, other arithmetic: 124 us -> none  [the longest x14 84.1 us: on_device(): factor = jnp.linalg.cholesky(gram_matrix)]
    pallas_call x0 -> x1, Pallas kernels: none -> 55.3 us  [inverse_factor(): pl.pallas_call(functools.partial(inverse_factor_kernel, block), out_shape...]
    dot_general x4 -> x1, matrix products: 54.5 us -> 13.7 us  [on_device(): lax.dot_general(flat_local, flat_local, contract_first, precision=lax.Pre...]
    reduce_sum x0 -> x3, other arithmetic: none -> 14.3 us  [precondition(): jnp.sum(flat_local * outer[None, :], axis=1).reshape(residue.shape)]
    another operation x17 -> x0, local copies, waits for them, and re-layouts: 11.3 us -> none
    another operation x13 -> x0, matrix products: 10 us -> none  [the longest x7 5.54 us: on_device(): jax.scipy.linalg.solve_triangular(factor, jnp.eye(sketch_rank, dtype=jnp....]
  transfers between devices with their start and end apart: 1 -> 1, of which waited for: 0 -> 0; matrix products, arithmetic and copies ran while one was open for 2% -> 3% of each run, Pallas kernels for 10% -> 14%
where the time goes in v2:
time: 323 us; the launch traced here: 322 us
  Pallas kernels  198 us (61%)
  blocking collectives  39.2 us (12%)
  matrix products  36.5 us (11%)
  other arithmetic  24.1 us (7%)
  between operations  20.3 us (6%)
  local copies, waits for them, and re-layouts  3.58 us (1%)
    pallas_call x4, Pallas kernels, sample_product(): pl.pallas_call(functools.partial(product_kernel, first, nf, ns, scale, ti...  143 us
    pallas_call x1, Pallas kernels, inverse_factor(): pl.pallas_call(functools.partial(inverse_factor_kernel, block), out_shape...  55.3 us
    dot_general x3, matrix products, precondition(): local_proj = jnp.dot(residue.reshape(-1), flat_local, precision=HIGHEST)  22.9 us
    psum x3, blocking collectives, precondition(): lax.psum(jnp.concatenate([local_proj, jnp.sum(residue * residue)[None]]),...  19.7 us
    psum x3, blocking collectives, on_device(): step_size = res_dot / lax.psum(jnp.sum(direction * hess_image), 'feat')  19.5 us
    reduce_sum x3, other arithmetic, precondition(): jnp.sum(flat_local * outer[None, :], axis=1).reshape(residue.shape)  14.3 us
    dot_general x1, matrix products, on_device(): lax.dot_general(flat_local, flat_local, contract_first, precision=lax.Pre...  13.7 us
  transfers between devices with their start and end apart: 1, of which 0 were waited for; matrix products, arithmetic and copies ran while one was open for 3% of the time, Pallas kernels for 14%

profile of v2, /device:TPU:0, one launch (start us, length us, event | category | flops | bytes accessed | tf_op | source)
XLA Modules:
  0.0 322.2 jit_solution(12224669528545214138)
XLA Ops:
  6.5 0.0 copy-start.1
  6.5 0.0 all-reduce.2.cloned.1.call-start
  6.5 13.7 %convolution_bitcast_fusion = f32[512,512]{1,0:T(8,128)} fusion(f32[10,512,512]{2,1,0:T(8,128)} %param.8), kind=kOutput, calls=%fused_computation.3 | convolution fusion | flops 8053063680 | bytes 11534336 | tf_op jit(solution)/shard_map/dot_general | solution.py:229
  20.2 0.0 all-reduce.2.cloned.1.call-update
  20.2 0.0 copy-done.1
  20.3 0.7 dynamic_slice.3
  21.0 0.0 copy-start.2
  21.0 46.1 %first_product.1 = (f32[10,512]{1,0:T(8,128)S(1)}, f32[10,4096]{1,0:T(8,128)S(1)}) custom-call(bf16[16384,512]{1,0:T(8,128)(2,1)} %refs_0_.7, bf16[10,512]{1,0:T(8,128)(2,1)S(1)} %convert_element_type.12.refs_1_, s32[1,4096]{1,0:T(1,128)S(1)} %bitcast.21), custom_call_target="tpu_custom_call" | custom-call | flops 335544320 | bytes 16777216 | tf_op jit(solution)/shard_map/first_product/pallas_call | solution.py:140
  67.1 0.6 multiply_reduce_fusion.14
  67.7 7.6 %fusion.4 = f32[1,512,1]{1,0,2:T(1,128)S(1)} fusion(f32[10,512,512]{2,1,0:T(8,128)} %param.8, f32[10,512,1]{1,0,2:T(8,128)S(1)} %get-tuple-element.25), kind=kOutput, calls=%fused_computation.30 | convolution fusion | flops 31457280 | bytes 10508288 | tf_op jit(solution)/shard_map/dot_general | solution.py:241
  75.3 0.7 pad_maximum_fusion
  76.0 5.7 %psum.49 = f32[513]{0:T(1024)S(1)} all-reduce(f32[513]{0:T(1024)S(1)} %pad_maximum_fusion), channel_id=1, replica_groups=mesh['samp'=8,'feat'=4] {'feat'}, use_global_device_ids=true, to_apply=%region_1.0 | all-reduce | flops 513 | bytes 4104 | tf_op jit(solution)/shard_map/psum | solution.py:242
  81.7 0.0 copy-done.2
  81.7 0.6 reduce_min.9
  82.9 0.0 all-reduce.2.cloned.1.call-done.gram_ref
  83.0 0.0 copy-start
  83.0 1.2 copy-done
  84.2 55.3 %inverse_factor.1 = f32[512,512]{1,0:T(8,128)S(1)} custom-call(f32[512,512]{1,0:T(8,128)S(1)} %copy-done), custom_call_target="tpu_custom_call" | custom-call | flops 1610612736 | bytes 2097152 | tf_op jit(solution)/shard_map/inverse_factor/pallas_call | solution.py:207
  139.5 0.2 multiply_reduce_fusion.8
  139.6 0.6 multiply_reduce_fusion.17
  140.2 0.1 multiply_reduce_fusion.7
  140.4 4.8 %multiply_reduce_fusion.2 = f32[10,512]{1,0:T(8,128)S(1)} fusion(f32[10,512,512]{2,1,0:T(8,128)} %param.8, f32[512]{0:T(512)S(1)} %multiply_reduce_fusion.7), kind=kLoop, calls=%fused_computation.2 | loop fusion | flops 5237760 | bytes 10508288 | tf_op jit(solution)/shard_map/reduce_sum | solution.py:245
  145.2 32.7 %curvature_product.3 = f32[10,512]{1,0:T(8,128)S(1)} custom-call(bf16[16384,512]{1,0:T(8,128)(2,1)} %refs_0_.7, bf16[10,512]{1,0:T(8,128)(2,1)S(1)} %get-tuple-element.23.refs_1_, f32[10,4096]{1,0:T(8,128)S(1)} %get-tuple-element.8.refs_2_), custom_call_target="tpu_custom_call" | custom-call | flops 335544320 | bytes 16777216 | tf_op jit(solution)/shard_map/curvature_product/pallas_call | solution.py:140
  177.9 0.6 multiply_reduce_fusion.13
  178.5 0.6 slice.18
  179.1 6.3 %psum.51 = f32[]{:T(128)} all-reduce(f32[]{:T(128)} %multiply_reduce_fusion.13), channel_id=1, replica_groups=mesh['samp'=8,'feat'=4] {'feat'}, use_global_device_ids=true, to_apply=%region_9.0 | all-reduce | flops 1 | bytes 8 | tf_op jit(solution)/shard_map/psum | solution.py:256
  187.3 0.6 multiply_reduce_fusion.12
  187.9 7.6 %fusion.2 = f32[1,512,1]{1,0,2:T(1,128)S(1)} fusion(f32[10,512,512]{2,1,0:T(8,128)} %param.8, f32[10,512,1]{1,0,2:T(8,128)S(1)} %bitcast.22), kind=kOutput, calls=%fused_computation.28 | convolution fusion | flops 31457280 | bytes 10508288 | tf_op jit(solution)/shard_map/dot_general | solution.py:241
  195.6 0.7 pad_maximum_fusion.1
  196.2 6.8 %psum.52 = f32[513]{0:T(1024)S(1)} all-reduce(f32[513]{0:T(1024)S(1)} %pad_maximum_fusion.1), channel_id=1, replica_groups=mesh['samp'=8,'feat'=4] {'feat'}, use_global_device_ids=true, to_apply=%region_11.0 | all-reduce | flops 513 | bytes 4104 | tf_op jit(solution)/shard_map/psum | solution.py:242
  203.0 0.5 slice.20
  203.5 0.2 multiply_reduce_fusion.6
  203.7 0.7 multiply_reduce_fusion.16
  205.7 0.1 multiply_reduce_fusion.5
  205.9 4.8 %multiply_reduce_fusion.1 = f32[10,512]{1,0:T(8,128)S(1)} fusion(f32[10,512,512]{2,1,0:T(8,128)} %param.8, f32[512]{0:T(512)S(1)} %multiply_reduce_fusion.5), kind=kLoop, calls=%fused_computation.1 | loop fusion | flops 5237760 | bytes 10508288 | tf_op jit(solution)/shard_map/reduce_sum | solution.py:245
  210.7 32.8 %curvature_product.4 = f32[10,512]{1,0:T(8,128)S(1)} custom-call(bf16[16384,512]{1,0:T(8,128)(2,1)} %refs_0_.7, bf16[10,512]{1,0:T(8,128)(2,1)S(1)} %get-tuple-element.15.refs_1_, f32[10,4096]{1,0:T(8,128)S(1)} %get-tuple-element.8.refs_2_), custom_call_target="tpu_custom_call" | custom-call | flops 335544320 | bytes 16777216 | tf_op jit(solution)/shard_map/curvature_product/pallas_call | solution.py:140
  243.5 0.6 multiply_reduce_fusion.11
  244.1 6.5 %psum.53 = f32[]{:T(128)} all-reduce(f32[]{:T(128)} %multiply_reduce_fusion.11), channel_id=1, replica_groups=mesh['samp'=8,'feat'=4] {'feat'}, use_global_device_ids=true, to_apply=%region_17.0 | all-reduce | flops 1 | bytes 8 | tf_op jit(solution)/shard_map/psum | solution.py:256
  251.3 0.6 multiply_reduce_fusion.10
  251.9 7.6 %fusion = f32[1,512,1]{1,0,2:T(1,128)S(1)} fusion(f32[10,512,512]{2,1,0:T(8,128)} %param.8, f32[10,512,1]{1,0,2:T(8,128)S(1)} %bitcast.23), kind=kOutput, calls=%fused_computation.26 | convolution fusion | flops 31457280 | bytes 10508288 | tf_op jit(solution)/shard_map/dot_general | solution.py:241
  259.5 0.7 pad_maximum_fusion.2
  260.2 7.2 %psum.54 = f32[513]{0:T(1024)S(1)} all-reduce(f32[513]{0:T(1024)S(1)} %pad_maximum_fusion.2), channel_id=1, replica_groups=mesh['samp'=8,'feat'=4] {'feat'}, use_global_device_ids=true, to_apply=%region_19.0 | all-reduce | flops 513 | bytes 4104 | tf_op jit(solution)/shard_map/psum | solution.py:242
  267.4 0.5 slice.22
  268.0 0.2 multiply_reduce_fusion.4
  268.1 0.7 multiply_reduce_fusion.15
  270.2 0.1 multiply_reduce_fusion.3
  270.3 4.8 %multiply_reduce_fusion = f32[10,512]{1,0:T(8,128)S(1)} fusion(f32[10,512,512]{2,1,0:T(8,128)} %param.8, f32[512]{0:T(512)S(1)} %multiply_reduce_fusion.3), kind=kLoop, calls=%fused_computation | loop fusion | flops 5237760 | bytes 10508288 | tf_op jit(solution)/shard_map/reduce_sum | solution.py:245
  275.1 31.5 %curvature_product.5 = f32[10,512]{1,0:T(8,128)S(1)} custom-call(bf16[16384,512]{1,0:T(8,128)(2,1)} %refs_0_.7, bf16[10,512]{1,0:T(8,128)(2,1)S(1)} %get-tuple-element.9.refs_1_, f32[10,4096]{1,0:T(8,128)S(1)} %get-tuple-element.8.refs_2_), custom_call_target="tpu_custom_call" | custom-call | flops 335544320 | bytes 16777216 | tf_op jit(solution)/shard_map/curvature_product/pallas_call | solution.py:140
  306.7 0.6 multiply_reduce_fusion.9
  307.3 6.8 %psum.55 = f32[]{:T(128)} all-reduce(f32[]{:T(128)} %multiply_reduce_fusion.9), channel_id=1, replica_groups=mesh['samp'=8,'feat'=4] {'feat'}, use_global_device_ids=true, to_apply=%region_25.0 | all-reduce | flops 1 | bytes 8 | tf_op jit(solution)/shard_map/psum | solution.py:256
  314.7 0.6 multiply_add_fusion
  (8 shorter events, 0.1 us)
Async XLA Ops:
  6.5 13.7 %copy-start.1 = (f32[10,512]{1,0:T(8,128)S(1)}, f32[10,512]{1,0:T(8,128)}, u32[]{:S(2)}) copy-start(f32[10,512]{1,0:T(8,128)} %param.7) | copy-start | bytes 61444
  6.5 76.4 %all-reduce.2.cloned.1.call-start = ((), (), s32[]{:S(2)}) async-start(), calls=%async_computation | async-start | bytes 2097152 | tf_op jit(solution)/shard_map/psum | solution.py:230
  21.0 60.7 %copy-start.2 = (f32[512]{0:T(512)S(1)}, f32[512]{0:T(512)}, u32[]{:S(2)}) copy-start(f32[512]{0:T(512)} %param.9) | copy-start | bytes 6148
  83.0 1.2 copy-start
Sparse Core Ops, SparseCore 0:
  20.4 46.3 all-reduce.1
